TPU v7x, 32 devices: a whole 2x2x4 slice. The times are simulated.
32 devices in a mesh: grp: 2 (over x), aux: 16 (over z, y, core).
Axes of the slice: x: 2, y: 2, z: 4, core: 2. Of those that a mesh axis runs over, the one named last changes fastest.
Arguments:
- three_index: bfloat16 [64, 256, 256], P('aux'), may hold values from -0.375 to 0.375
- relaxed: bfloat16 [512, 256], P('grp'), parts along dimension 0, may hold values from -0.375 to 0.375
- plus_amplitude: bfloat16 [512, 256], P('grp'), parts along dimension 0, may hold values from -0.375 to 0.375
- minus_amplitude: bfloat16 [512, 256], P('grp'), parts along dimension 0, may hold values from -0.375 to 0.375
- ground: bfloat16 [256, 256], replicated, may hold values from -0.375 to 0.375
- integral_grad: bfloat16 [3, 64, 512, 256], P(None, None, 'aux'), may hold values from -0.09375 to 0.09375
- metric_grad: bfloat16 [3, 64, 64], P(None, 'aux'), may hold values from -0.5 to 0.5
- function_atom: int32 [256], replicated, may hold values from 0 to 31, never falling along the last dimension, each value on 1 to 16 neighbouring positions
- aux_center: int32 [64], P('aux'), may hold values from 0 to 31, never falling along the last dimension, each value on 1 to 4 neighbouring positions
- block_list: int32 [512], replicated, may hold values from 0 to 255, as said below
- block_count: int32 [16], replicated, may hold values from 0 to 32, as said below
Outputs:
- gradient: float32 [3, 64], P(None, 'grp'), parts along dimension 1
There are 2 independent parts, one for each index of `grp`. A program takes and returns all parts, laid end to end along the dimension named above; an argument that names none is the same for every part. Nothing has to cross between parts.
Inputs may be any that keep to these rules, and one draw needn't show every extreme that they name: block_count[d] is the number of live slots of owner d; the counts sum to 256, and at least one owner has 32. `block_list`: slot s of owner d is entry d * 32 + s and is live when s < block_count[d]; each tile pair i * 16 + j is held by exactly one live slot; slots that are not live hold arbitrary tile pairs.
All inputs are finite; a program needn't handle non-finite values.
Results may differ from a plain program's by a relative error of at most 0.0032.
Values may be sent and summed in bfloat16 or wider, within the bound.
No kernel may reach another device: no remote copies, remote signals or barrier semaphores. Data moves between devices by JAX's collectives and lax.ppermute only.
A program may use at most 64 MiB of HBM per device.

v0:
```python
import jax
import jax.numpy as jnp
from jax import lax
from jax.sharding import PartitionSpec as P

TILE = 16
NATOM = 32


def on_device(
    three_index,
    relaxed,
    plus_amplitude,
    minus_amplitude,
    ground,
    integral_grad,
    metric_grad,
    function_atom,
    aux_center,
    block_list,
    block_count,
):
    highest = lax.Precision.HIGHEST
    aux_local = three_index.shape[0]
    basis_count = three_index.shape[1]
    tile_count = basis_count // TILE
    slot_depth = integral_grad.shape[2]
    slot_total = block_list.shape[0]
    fitted = jnp.einsum("pab,ab->p", three_index, relaxed, preferred_element_type=jnp.float32)
    stacked = jnp.concatenate([plus_amplitude, minus_amplitude, ground], 0)
    halves = jnp.einsum(
        "ab,pbc->pac", stacked, three_index, preferred_element_type=jnp.float32
    ).astype(jnp.bfloat16)
    paired_half = halves[:, : 2 * basis_count].reshape(aux_local, 2, basis_count, basis_count)
    paired_half = jnp.concatenate([paired_half[:, 0], paired_half[:, 1]], axis=2)
    ground_half = halves[:, 2 * basis_count :]
    partners = jnp.concatenate([plus_amplitude, -minus_amplitude], axis=1)
    exchange_part = jnp.einsum(
        "pab,cb->pac", paired_half, partners, preferred_element_type=jnp.float32
    )
    crossed = jnp.einsum("pab,bc->pac", ground_half, relaxed, preferred_element_type=jnp.float32)
    triple = (
        fitted[:, None, None] * relaxed.astype(jnp.float32)[None]
        + exchange_part
        + crossed
        + jnp.swapaxes(crossed, 1, 2)
    )
    triple = triple.astype(jnp.bfloat16)
    blocked = triple.reshape(aux_local, tile_count, TILE, tile_count, TILE).transpose(0, 1, 3, 2, 4)
    blocked = blocked.reshape(aux_local, tile_count * tile_count, TILE * TILE)
    chosen = jnp.take(blocked, block_list, axis=1)
    slot_ids = jnp.arange(slot_total, dtype=jnp.int32)
    live_mask = (slot_ids % slot_depth < block_count[slot_ids // slot_depth]).astype(jnp.float32)
    arrived = lax.all_to_all(chosen, "aux", split_axis=1, concat_axis=0, tiled=True)
    first_slot = lax.axis_index("aux") * slot_depth
    tile_ids = lax.dynamic_slice_in_dim(block_list, first_slot, slot_depth)
    slot_mask = lax.dynamic_slice_in_dim(live_mask, first_slot, slot_depth)
    contracted = jnp.einsum(
        "pgf,kpgf->kgf", arrived, integral_grad, preferred_element_type=jnp.float32
    )
    slot_count = tile_ids.shape[0]
    row_sums = contracted.reshape(3, slot_count, TILE, TILE).sum(axis=3) * slot_mask[None, :, None]
    function_ids = (tile_ids // tile_count)[:, None] * TILE + jnp.arange(TILE, dtype=jnp.int32)[
        None, :
    ]
    atom_table = (
        function_atom[function_ids][:, :, None] == jnp.arange(NATOM, dtype=jnp.int32)[None, None, :]
    ).astype(jnp.float32)
    three_part = 2.0 * jnp.einsum("kgm,gma->ka", row_sums, atom_table, precision=highest)
    all_fitted = lax.all_gather(fitted, "aux", axis=0, tiled=True)
    coupling = jnp.einsum(
        "kpq,q->kp", metric_grad.astype(jnp.float32), all_fitted, precision=highest
    )
    aux_table = (aux_center[:, None] == jnp.arange(NATOM, dtype=jnp.int32)[None, :]).astype(
        jnp.float32
    )
    metric_part = jnp.einsum("kp,pa->ka", coupling * fitted[None, :], aux_table, precision=highest)
    return lax.psum(three_part - metric_part, "aux")


def solution(mesh):
    in_specs = (
        P("aux", None, None),
        P("grp", None),
        P("grp", None),
        P("grp", None),
        P(),
        P(None, None, "aux", None),
        P(None, "aux", None),
        P(),
        P("aux"),
        P(),
        P(),
    )
    out_specs = P(None, "grp")
    return jax.shard_map(
        on_device, mesh=mesh, in_specs=in_specs, out_specs=out_specs, check_vma=False
    )
```

profile of v0, /device:TPU:0, one launch (start us, length us, event | category | flops | bytes accessed | tf_op | source)
XLA Modules:
  0.0 119.7 jit_solution(17670021363365028496)
XLA Ops:
  0.0 1.8 %fusion = bf16[4,768,256]{2,1,0:T(8,128)(2,1)S(1)} fusion(bf16[4,256,256]{2,1,0:T(8,128)(2,1)} %param.11, bf16[256,256]{1,0:T(8,128)(2,1)} %param.15, bf16[256,256]{1,0:T(8,128)(2,1)} %param.14, bf16[256,256]{1,0:T(8,128)(2,1)} %param.13), kind=kOutput, calls=%fused_computation.5 | convolution fusion | flops 404619264 | bytes 2490368 | tf_op jit(solution)/shard_map/ab,pbc->pac/dot_general | solution.py:31
  1.9 0.0 copy-start.6
  1.9 0.0 copy-start.10
  1.9 0.1 slice.37
  2.0 0.3 fusion.8
  2.3 0.5 copy-done.6
  2.8 0.7 neg.3
  3.5 0.0 copy-start.4
  3.5 0.9 slice_bitcast_fusion.1
  4.3 0.3 copy.42
  4.7 1.9 %convolution_bitcast_fusion.1 = f32[4]{0:T(128)S(1)} fusion(bf16[4,256,256]{2,1,0:T(8,128)(2,1)S(1)} %copy-done.4, bf16[256,256,1]{1,0,2:T(8,128)(2,1)} %bitcast.80), kind=kOutput, calls=%fused_computation.13 | convolution fusion | flops 524288 | bytes 655376 | tf_op jit(solution)/shard_map/pab,ab->p/dot_general | solution.py:29
  6.6 0.5 copy-done.11
  7.1 0.5 fusion.3
  7.6 4.2 %reshape.108 = bf16[4,16,16,16,16]{4,3,2,1,0:T(8,128)(2,1)} reshape(bf16[4,256,256]{2,1,0:T(8,128)(2,1)S(1)} %fusion.3) | data formatting | bytes 1048576 | tf_op jit(solution)/shard_map/reshape | solution.py:49
  11.7 5.2 %copy.74 = bf16[4,16,16,16,16]{4,2,3,1,0:T(8,128)(2,1)} copy(bf16[4,16,16,16,16]{4,3,2,1,0:T(8,128)(2,1)} %reshape.108) | data formatting | bytes 1048576 | tf_op jit(solution)/shard_map/reshape | solution.py:49
  17.0 5.5 %reshape.109 = bf16[4,256,256]{2,1,0:T(8,128)(2,1)S(1)} reshape(bf16[4,16,16,16,16]{4,3,2,1,0:T(8,128)(2,1)} %bitcast.77) | data formatting | bytes 1048576 | tf_op jit(solution)/shard_map/reshape | solution.py:50
  22.5 0.4 copy.44
  22.9 2.4 %gather_fusion = bf16[512,4,256]{2,1,0:T(4,128)(2,1)S(1)} fusion(bf16[4,256,256]{2,0,1:T(4,128)(2,1)S(1)} %copy.44, s32[1024]{0:T(1024)S(1)} %pad_clamp_fusion.1), kind=kCustom, calls=%fused_computation | custom fusion | bytes 2099200 | tf_op jit(solution)/shard_map/jit(_take)/gather | solution.py:51
  25.3 0.0 copy-start.9
  25.3 0.0 copy-start.1
  25.3 2.7 %select_bitcast_fusion = bf16[4,512,256]{2,0,1:T(4,128)(2,1)} fusion(bf16[512,4,256]{2,1,0:T(4,128)(2,1)S(1)} %gather_fusion, pred[512]{0:T(512)(128)(4,1)S(1)} %compare_and_fusion), kind=kLoop, calls=%fused_computation.18 | loop fusion | flops 524288 | bytes 2097664 | tf_op jit(solution)/shard_map/jit(_take)/select_n | solution.py:51
  28.0 7.4 %all-to-all-start = ((bf16[4,512,256]{2,0,1:T(4,128)(2,1)}), bf16[4,512,256]{2,0,1:T(4,128)(2,1)S(1)}, u32[]{:S(2)}, u32[]{:S(2)}) async-start(bf16[4,512,256]{2,0,1:T(4,128)(2,1)} %select_bitcast_fusion), calls=%async_computation | async-start | bytes 2097152 | tf_op jit(solution)/shard_map/all_to_all | solution.py:54
  35.7 0.7 fusion.34
  36.5 4.3 %compare_select_fusion.2 = s32[512,1]{0,1:T(1,128)S(1)} fusion(s32[]{:T(128)} %bitcast.30, s32[]{:T(128)} %bitcast.31, s32[]{:T(128)} %bitcast.32, s32[]{:T(128)} %bitcast.33, s32[]{:T(128)} %bitcast.34, s32[]{:T(128)} %bitcast.36, s32[]{:T(128)} %bitcast.35), kind=kLoop, calls=%fused_computation.49 | loop fusion | flops 11776 | bytes 2076 | tf_op jit(solution)/shard_map/gather | solution.py:53
  40.8 5.7 %fusion.25 = f32[512]{0:T(512)S(1)} fusion(pred[512]{0:T(512)(128)(4,1)S(1)} %compare_reduce_fusion, pred[512]{0:T(512)(128)(4,1)S(1)} %compare_reduce_fusion.1, pred[512]{0:T(512)(128)(4,1)S(1)} %compare_reduce_fusion.2, pred[512]{0:T(512)(128)(4,1)S(1)} %compare_reduce_fusion.3, pred[512]{0:T(512)(128)(4,1)S(1)} %compare_reduce_fusion.4, ...), kind=kLoop, calls=%fused_computation.73 | loop fusion | flops 8704 | bytes 8740 | tf_op jit(solution)/shard_map/convert_element_type | solution.py:53
  46.4 0.1 dynamic_slice.6
  46.5 0.1 fusion.28
  46.6 0.1 compare_select_fusion
  46.7 0.1 reshape.144
  46.8 0.0 copy-start.14
  46.8 3.5 %gather_fusion.1 = s32[512]{0:T(512)S(1)} fusion(s32[256]{0:T(256)S(1)} %copy-done.1, s32[1024]{0:T(1024)S(1)} %pad_clamp_fusion), kind=kCustom, calls=%fused_computation.1 | custom fusion | bytes 6144 | tf_op jit(solution)/shard_map/gather | solution.py:67
  50.3 0.1 reshape.143
  50.4 0.1 copy.46
  50.5 0.6 dynamic-slice
  51.7 0.2 dynamic-update-slice
  52.0 33.9 %all-reduce = f32[64]{0:T(128)S(1)} all-reduce(f32[64]{0:T(128)S(1)} %dynamic-update-slice), channel_id=1, replica_groups=mesh['grp'=2,'aux'=16] {'aux'}, use_global_device_ids=true, to_apply=%add | all-reduce | flops 64 | bytes 512
  85.9 0.1 fusion.29
  86.0 0.0 all-to-all-done
  86.1 0.2 copy.59
  86.3 0.0 copy-start.2
  86.3 0.3 bitcast_convert_fusion
  86.6 1.5 %copy-done.2 = bf16[3,64,32,256]{3,2,1,0:T(8,128)(2,1)S(1)} copy-done((bf16[3,64,32,256]{3,2,1,0:T(8,128)(2,1)S(1)}, bf16[3,64,32,256]{3,2,1,0:T(8,128)(2,1)}, u32[]{:S(2)}) %copy-start.2) | copy-done | bytes 3145752
  88.2 0.7 multiply_reduce_fusion
  88.9 0.2 copy.57
  89.1 0.1 bitcast_reduce_fusion
  89.2 0.3 fusion.4
  89.5 0.2 convolution_subtract_fusion
  89.7 30.1 %psum.7 = f32[3,32]{1,0:T(4,128)} all-reduce(f32[3,32]{1,0:T(4,128)S(1)} %convolution_subtract_fusion), channel_id=1, replica_groups=mesh['grp'=2,'aux'=16] {'aux'}, use_global_device_ids=true, to_apply=%region_1.2 | all-reduce | flops 96 | bytes 768 | tf_op jit(solution)/shard_map/psum | solution.py:78
  (36 shorter events, 0.4 us)
Async XLA Ops:
  0.0 85.9 %copy-start = (bf16[3,4,64]{2,1,0:T(4,128)(2,1)S(1)}, bf16[3,4,64]{2,1,0:T(4,128)(2,1)}, u32[]{:S(2)}) copy-start(bf16[3,4,64]{2,1,0:T(4,128)(2,1)} %param.17) | copy-start | bytes 4612
  0.0 2.0 %copy-start.8 = (bf16[256,256]{1,0:T(8,128)(2,1)S(1)}, bf16[256,256]{1,0:T(8,128)(2,1)}, u32[]{:S(2)}) copy-start(bf16[256,256]{1,0:T(8,128)(2,1)} %param.12) | copy-start | bytes 393220
  1.9 0.9 copy-start.6
  1.9 1.6 %copy-start.10 = (s32[512]{0:T(512)S(1)}, s32[512]{0:T(512)}, u32[]{:S(2)}) copy-start(s32[512]{0:T(512)} %param.20) | copy-start | bytes 6148
  3.5 1.2 %copy-start.4 = (bf16[4,256,256]{2,1,0:T(8,128)(2,1)S(1)}, bf16[4,256,256]{2,1,0:T(8,128)(2,1)}, u32[]{:S(2)}) copy-start(bf16[4,256,256]{2,1,0:T(8,128)(2,1)} %param.11) | copy-start | bytes 1572868
  4.3 2.8 %copy-start.5 = (bf16[256,256]{1,0:T(8,128)(2,1)S(1)}, bf16[256,256]{1,0:T(8,128)(2,1)}, u32[]{:S(2)}) copy-start(bf16[256,256]{1,0:T(8,128)(2,1)} %param.13) | copy-start | bytes 393220
  4.7 2.4 %copy-start.3 = (bf16[4,256,256]{2,1,0:T(8,128)(2,1)S(1)}, bf16[4,256,256]{2,1,0:T(8,128)(2,1)}, u32[]{:S(2)}) copy-start(bf16[4,256,256]{2,1,0:T(8,128)(2,1)} %get-tuple-element.6) | copy-start | bytes 1572868
  4.7 2.4 %copy-start.7 = (bf16[256,256]{1,0:T(8,128)(2,1)S(1)}, bf16[256,256]{1,0:T(8,128)(2,1)}, u32[]{:S(2)}) copy-start(bf16[256,256]{1,0:T(8,128)(2,1)} %neg.3) | copy-start | bytes 393220
  6.6 0.5 copy-start.11
  25.3 10.4 %copy-start.9 = (s32[16]{0:T(128)S(1)}, s32[16]{0:T(128)}, u32[]{:S(2)}) copy-start(s32[16]{0:T(128)} %param.21) | copy-start | bytes 196
  25.3 21.4 %copy-start.1 = (s32[256]{0:T(256)S(1)}, s32[256]{0:T(256)}, u32[]{:S(2)}) copy-start(s32[256]{0:T(256)} %param.18) | copy-start | bytes 3076
  28.0 58.0 %all-to-all-start = ((bf16[4,512,256]{2,0,1:T(4,128)(2,1)}), bf16[4,512,256]{2,0,1:T(4,128)(2,1)S(1)}, u32[]{:S(2)}, u32[]{:S(2)}) async-start(bf16[4,512,256]{2,0,1:T(4,128)(2,1)} %select_bitcast_fusion), calls=%async_computation | async-start | bytes 2097152 | tf_op jit(solution)/shard_map/all_to_all | solution.py:54
  46.8 3.7 %copy-start.14 = (u32[32]{0:T(128)S(1)}, u32[32]{0:T(128)}, u32[]{:S(2)}) copy-start(u32[32]{0:T(128)} %constant.97) | copy-start | bytes 388
  46.8 4.9 %copy-start.12 = (f32[4]{0:T(128)S(1)}, f32[4]{0:T(128)}, u32[]{:S(2)}) copy-start(f32[4]{0:T(128)} %copy-done.11) | copy-start | bytes 52
  86.3 1.9 %copy-start.2 = (bf16[3,64,32,256]{3,2,1,0:T(8,128)(2,1)S(1)}, bf16[3,64,32,256]{3,2,1,0:T(8,128)(2,1)}, u32[]{:S(2)}) copy-start(bf16[3,64,32,256]{3,2,1,0:T(8,128)(2,1)} %param.16) | copy-start | bytes 9437188
  88.2 1.3 %copy-start.13 = (s32[4]{0:T(128)S(1)}, s32[4]{0:T(128)}, u32[]{:S(2)}) copy-start(s32[4]{0:T(128)} %param.19) | copy-start | bytes 52
where the time goes:
time: 120 us
  blocking collectives  64 us (53%)
  local copies, waits for them, and re-layouts  27.3 us (23%)
  other arithmetic  15 us (12%)
  starting transfers between devices  7.41 us (6%)
  matrix products  5.13 us (4%)
    unnamed x1, blocking collectives  33.9 us
    psum x1, blocking collectives, on_device(): return lax.psum(three_part - metric_part, 'aux')  30.1 us
    reshape x2, local copies, waits for them, and re-layouts, on_device(): triple.reshape(aux_local, tile_count, TILE, tile_count, TILE)  9.39 us
    all_to_all x1, starting transfers between devices, on_device(): lax.all_to_all(chosen, 'aux', split_axis=1, concat_axis=0, tiled=True)  7.41 us
    reshape x2, local copies, waits for them, and re-layouts, on_device(): blocked = blocked.reshape(aux_local, tile_count * tile_count, TILE * TILE)  5.89 us
    convert_element_type x1, other arithmetic, on_device(): (slot_ids % slot_depth < block_count[slot_ids // slot_depth]).astype(jnp....  5.67 us
    gather x10, other arithmetic, on_device(): block_count[slot_ids // slot_depth]  4.61 us
    gather x3, local copies, waits for them, and re-layouts, on_device(): function_atom[function_ids][:, :, None]  3.67 us
  transfers between devices with their start and end apart: 1, of which 0 were waited for; matrix products, arithmetic and copies ran while one was open for 13% of the time, Pallas kernels for 0%

commit v1 on v0

v1 whole, which is shorter than its diff:
```python
import functools

import jax
import jax.numpy as jnp
from jax import lax
from jax.experimental import pallas as pl
from jax.experimental.pallas import tpu as pltpu
from jax.sharding import PartitionSpec as P

TILE = 16
NATOM = 32
LANES = 128

f32 = jnp.float32
bf16 = jnp.bfloat16


def dot(a, b, ca=1, cb=0):
    return lax.dot_general(a, b, (((ca,), (cb,)), ((), ())), preferred_element_type=f32)


def iota(shape, dim):
    return lax.broadcasted_iota(jnp.int32, shape, dim)


def swap_blocks(quadrant):
    half = LANES // TILE
    blocks = [quadrant[u * TILE : (u + 1) * TILE] for u in range(half)]
    lane = iota((TILE, LANES), 1) // TILE
    step = half // 2
    while step:
        upper = (lane // step) % 2 == 1
        for u in range(half):
            if u & step:
                continue
            low, high = blocks[u], blocks[u + step]
            blocks[u] = jnp.where(upper, pltpu.roll(high, step * TILE, 1), low)
            blocks[u + step] = jnp.where(upper, high, pltpu.roll(low, LANES - step * TILE, 1))
        step //= 2
    return jnp.concatenate(blocks, axis=0)


def density_kernel(owners, depth, *refs):
    slabs_hbm, r_hbm, x_hbm, y_hbm, g_hbm, list_hbm, out_ref, weight_ref = refs[:8]
    slab_ref, r_ref, x_ref, y_ref, g_ref, list_ref, left_ref, fixed_ref, rows_ref, pick_ref, sem = refs[8:]
    aux_local = slabs_hbm.shape[0]
    size = r_ref.shape[0]
    tiles = size // TILE
    copies = [
        pltpu.make_async_copy(source, target, sem.at[k])
        for k, (source, target) in enumerate(
            ((list_hbm, list_ref), (x_hbm, x_ref), (y_hbm, y_ref), (g_hbm, g_ref), (r_hbm, r_ref))
        )
    ]
    copies += [pltpu.make_async_copy(slabs_hbm.at[p], slab_ref.at[p], sem.at[5 + p]) for p in range(aux_local)]
    for copy in copies:
        copy.start()
    me = lax.axis_index("aux")
    row = iota((size, size), 0)
    spread = jnp.where((row % tiles) * TILE + row // tiles == iota((size, size), 1), 1.0, 0.0).astype(bf16)
    copies[0].wait()
    tile_ids = list_ref[...]
    places = (tile_ids % tiles) * tiles + tile_ids // tiles
    total = places.shape[1]
    pick_ref[...] = jnp.where(iota((tiles * tiles, total), 0) == places, 1.0, 0.0).T.astype(bf16)
    copies[1].wait()
    left_ref[0:size, :] = dot(spread, x_ref[...]).astype(bf16)
    copies[2].wait()
    left_ref[size : 2 * size, :] = -dot(spread, y_ref[...]).astype(bf16)
    copies[3].wait()
    left_ref[2 * size : 3 * size, :] = dot(spread, g_ref[...]).astype(bf16)
    left_ref[3 * size :, :] = g_ref[...]
    copies[4].wait()
    fixed_ref[...] = dot(spread, r_ref[...], 1, 1).astype(bf16)
    rows_ref[...] = dot(spread, r_ref[...])
    width = weight_ref.shape[1]
    lanes = iota((8, width), 1)
    weights_row = jnp.zeros((8, width), f32)
    for p in range(aux_local):
        copies[5 + p].wait()
        slab = slab_ref[p]
        product = slab.astype(f32) * r_ref[...].astype(f32)
        weight = jnp.sum(jnp.sum(product, axis=0, keepdims=True), axis=1, keepdims=True)
        weights_row = jnp.where(lanes == me * aux_local + p, weight, weights_row)
        halves = dot(left_ref[...], slab).astype(bf16)
        wide = jnp.concatenate([halves[0:size], halves[size : 2 * size], fixed_ref[...]], axis=1)
        right = jnp.concatenate([x_ref[...], y_ref[...], halves[3 * size :]], axis=1)
        triple = dot(wide, right, 1, 1) + dot(halves[2 * size : 3 * size], r_ref[...]) + weight * rows_ref[...]
        parts = []
        for h in range(2):
            parts.append(
                jnp.concatenate(
                    [
                        swap_blocks(triple[v * LANES : (v + 1) * LANES, h * LANES : (h + 1) * LANES])
                        for v in range(2)
                    ],
                    axis=1,
                )
            )
        blocked = jnp.concatenate(parts, axis=0).astype(bf16)
        chosen = dot(pick_ref[...], blocked).astype(bf16)
        for d in range(owners):
            out_ref[d, p * depth : (p + 1) * depth, :] = chosen[d * depth : (d + 1) * depth]
    weight_ref[...] = weights_row


def prepare_kernel(depth, *refs):
    grad_hbm, metric_hbm, atoms_hbm, centers_hbm, list_hbm, count_hbm, weight_ref = refs[:7]
    components = grad_hbm.shape[0]
    grad_refs = refs[7 : 7 + components]
    at_ref, message_ref = refs[7 + components : 9 + components]
    metric_ref, atoms_ref, centers_ref, list_ref, count_ref, table_ref, sem = refs[9 + components :]
    copies = [
        pltpu.make_async_copy(source, target, sem.at[k])
        for k, (source, target) in enumerate(
            (
                (atoms_hbm, atoms_ref),
                (list_hbm, list_ref),
                (count_hbm, count_ref),
                (metric_hbm, metric_ref),
                (centers_hbm, centers_ref),
                *((grad_hbm.at[c], grad_refs[c]) for c in range(components)),
            )
        )
    ]
    for copy in copies:
        copy.start()
    _, aux_local, aux_total = metric_ref.shape
    size = at_ref.shape[1]
    tiles = size // TILE
    me = lax.axis_index("aux")
    wide = iota((size, size), 1)
    deep = iota((size, size), 0)
    expand = jnp.where(deep % TILE == wide // TILE, 1.0, 0.0).astype(bf16)
    mine = iota((tiles, size), 1) // TILE == iota((tiles, size), 0)
    copies[0].wait()
    atoms = jnp.where(mine, jnp.broadcast_to(atoms_ref[...], (tiles, size)).astype(f32), 0.0).astype(bf16)
    table_ref[...] = dot(atoms, expand).astype(jnp.int32)
    copies[1].wait()
    copies[2].wait()
    count = count_ref[me]
    for g in range(depth):
        i = list_ref[me * depth + g] // tiles
        at_ref[g : g + 1, :] = jnp.where(g < count, table_ref[pl.ds(i, 1), :], -1)
    copies[3].wait()
    copies[4].wait()
    message_ref[...] = jnp.zeros(message_ref.shape, f32)
    weights = weight_ref[0:1, :]
    lanes = iota(weights.shape, 1)
    lane = iota((1, LANES), 1)
    for p in range(aux_local):
        weight = jnp.sum(jnp.where(lanes == me * aux_local + p, weights, 0.0), axis=1, keepdims=True)
        center = jnp.where(lane == 0, centers_ref[p].astype(f32), 0.0)
        for c in range(components):
            k = c * aux_local + p
            message_ref[k : k + 1, 0:aux_total] = weight * metric_ref[c, p : p + 1, :].astype(f32)
            message_ref[k : k + 1, aux_total : aux_total + 1] = center[:, 0:1]
    k = components * (aux_local + 1)
    message_ref[k : k + 1, :] = weights
    for copy in copies[5:]:
        copy.wait()


def gradient_kernel(depth, arrived, *refs):
    grad_refs, (at_ref, message_ref, out_ref) = refs[:-3], refs[-3:]
    components, size = len(grad_refs), arrived.shape[2]
    owners, rows, _ = arrived.shape
    aux_local = rows // depth
    sums = [jnp.zeros((depth, size), f32) for _ in range(components)]
    for d in range(owners):
        for p in range(aux_local):
            tile = arrived[d, p * depth : (p + 1) * depth, :].astype(f32)
            for c in range(components):
                sums[c] = sums[c] + tile * grad_refs[c][d * aux_local + p].astype(f32)
    at = at_ref[...]
    lane_atom = iota((1, message_ref.shape[1]), 1)
    lines = []
    for c in range(components):
        line = jnp.zeros(lane_atom.shape, f32)
        for a in range(NATOM):
            picked = jnp.sum(jnp.where(at == a, sums[c], 0.0), axis=0, keepdims=True)
            value = jnp.sum(picked, axis=1, keepdims=True)
            line = jnp.where(lane_atom == a, 2.0 * value, line)
        lines.append(line)
    base = components * aux_local
    message = message_ref[...]
    row = iota(message.shape, 0)
    for c in range(components):
        message = jnp.where(row == base + c, lines[c], message)
    for d in range(owners):
        out_ref[d] = message


def finish_kernel(components, aux_local, aux_total, arrived, out_ref):
    base = components * aux_local
    total = jnp.sum(arrived[...], axis=0)
    fitted = total[base + components : base + components + 1]
    terms = arrived[:, 0:base, :]
    coupling = jnp.sum(terms * fitted[None], axis=2, keepdims=True)
    center = terms[:, :, aux_total : aux_total + 1].astype(jnp.int32)
    lane = iota((1, 1, NATOM), 2)
    spread = jnp.sum(jnp.where(center == lane, coupling, 0.0), axis=0)
    for c in range(components):
        metric_part = jnp.sum(spread[c * aux_local : (c + 1) * aux_local], axis=0, keepdims=True)
        out_ref[c : c + 1, :] = total[base + c : base + c + 1, 0:NATOM] - metric_part


def on_device(
    owners,
    three_index,
    relaxed,
    plus_amplitude,
    minus_amplitude,
    ground,
    integral_grad,
    metric_grad,
    function_atom,
    aux_center,
    block_list,
    block_count,
):
    aux_local, size, _ = three_index.shape
    components, aux_total, depth, _ = integral_grad.shape
    tiles = size // TILE
    slots = block_list.shape[0]
    width = (aux_total // LANES + 1) * LANES
    lines = (components * (aux_local + 1) + 8) // 8 * 8
    vmem = pl.BlockSpec(memory_space=pltpu.VMEM)
    hbm = pl.BlockSpec(memory_space=pltpu.HBM)
    payload, weights = pl.pallas_call(
        functools.partial(density_kernel, owners, depth),
        out_shape=[
            jax.ShapeDtypeStruct((owners, aux_local * depth, size), bf16),
            jax.ShapeDtypeStruct((8, width), f32),
        ],
        in_specs=[hbm] * 6,
        out_specs=[vmem] * 2,
        scratch_shapes=[
            pltpu.VMEM((aux_local, size, size), bf16),
            pltpu.VMEM((size, size), bf16),
            pltpu.VMEM((size, size), bf16),
            pltpu.VMEM((size, size), bf16),
            pltpu.VMEM((size, size), bf16),
            pltpu.VMEM((1, slots), jnp.int32),
            pltpu.VMEM((4 * size, size), bf16),
            pltpu.VMEM((size, size), bf16),
            pltpu.VMEM((size, size), f32),
            pltpu.VMEM((slots, tiles * tiles), bf16),
            pltpu.SemaphoreType.DMA((5 + aux_local,)),
        ],
        compiler_params=pltpu.CompilerParams(vmem_limit_bytes=63 << 20),
        cost_estimate=pl.CostEstimate(flops=1 << 30, bytes_accessed=1 << 21, transcendentals=0),
        name="density",
    )(three_index, relaxed, plus_amplitude, minus_amplitude, ground, block_list[None, :])
    arrived = lax.all_to_all(payload, "aux", 0, 0, tiled=True)
    *grads, at, message = pl.pallas_call(
        functools.partial(prepare_kernel, depth),
        out_shape=[
            *[jax.ShapeDtypeStruct(integral_grad.shape[1:], bf16)] * components,
            jax.ShapeDtypeStruct((depth, size), jnp.int32),
            jax.ShapeDtypeStruct((lines, width), f32),
        ],
        in_specs=[hbm] * 6 + [vmem],
        out_specs=[vmem] * (2 + components),
        scratch_shapes=[
            pltpu.VMEM(metric_grad.shape, bf16),
            pltpu.VMEM((1, size), jnp.int32),
            pltpu.SMEM(aux_center.shape, jnp.int32),
            pltpu.SMEM(block_list.shape, jnp.int32),
            pltpu.SMEM(block_count.shape, jnp.int32),
            pltpu.VMEM((tiles, size), jnp.int32),
            pltpu.SemaphoreType.DMA((5 + components,)),
        ],
        compiler_params=pltpu.CompilerParams(vmem_limit_bytes=12 << 20),
        cost_estimate=pl.CostEstimate(flops=1 << 30, bytes_accessed=1 << 22, transcendentals=0),
        name="prepare",
    )(integral_grad, metric_grad, function_atom[None, :], aux_center, block_list, block_count, weights)
    partial = pl.pallas_call(
        functools.partial(gradient_kernel, depth),
        out_shape=jax.ShapeDtypeStruct((owners, lines, width), f32),
        in_specs=[vmem] * (3 + components),
        out_specs=vmem,
        compiler_params=pltpu.CompilerParams(vmem_limit_bytes=16 << 20),
        name="gradient",
    )(arrived, *grads, at, message)
    partial = lax.all_to_all(partial, "aux", 0, 0, tiled=True)
    return pl.pallas_call(
        functools.partial(finish_kernel, components, aux_local, aux_total),
        out_shape=jax.ShapeDtypeStruct((components, NATOM), f32),
        in_specs=[vmem],
        out_specs=vmem,
        name="finish",
    )(partial)


def solution(mesh):
    in_specs = (
        P("aux", None, None),
        P("grp", None),
        P("grp", None),
        P("grp", None),
        P(),
        P(None, None, "aux", None),
        P(None, "aux", None),
        P(),
        P("aux"),
        P(),
        P(),
    )
    out_specs = P(None, "grp")
    return jax.shard_map(
        functools.partial(on_device, mesh.shape["aux"]),
        mesh=mesh,
        in_specs=in_specs,
        out_specs=out_specs,
        check_vma=False,
    )
```

time: 120 us -> 56.8 us (0.47)
  blocking collectives: 64 us -> 14.6 us
  local copies, waits for them, and re-layouts: 27.3 us -> 4.79 us
  waiting for transfers between devices: 0.01 us -> 18.3 us
  other arithmetic: 15 us -> 0 us
  Pallas kernels: 0 us -> 11.3 us
  matrix products: 5.13 us -> 0 us
    unnamed x1 -> x0, blocking collectives: 33.9 us -> none
    psum x1 -> x0, blocking collectives: 30.1 us -> none  [on_device(): return lax.psum(three_part - metric_part, 'aux')]
    all_to_all x1, waiting for transfers between devices: 0.01 us -> 18.3 us  [on_device(): arrived = lax.all_to_all(payload, 'aux', 0, 0, tiled=True)]
    reshape x4 -> x0, local copies, waits for them, and re-layouts: 15.3 us -> none  [the longest x2 9.39 us: on_device(): triple.reshape(aux_local, tile_count, TILE, tile_count, TILE)]
    all_to_all x0 -> x1, blocking collectives: none -> 14.6 us  [on_device(): partial = lax.all_to_all(partial, 'aux', 0, 0, tiled=True)]
    pallas_call x0 -> x4, Pallas kernels: none -> 11.3 us  [the longest x1 7.61 us: on_device(): pl.pallas_call(functools.partial(density_kernel, owners, depth), out_shap...]
    gather x5 -> x0, local copies, waits for them, and re-layouts: 6.78 us -> none  [the longest x3 3.67 us: on_device(): function_atom[function_ids][:, :, None]]
    convert_element_type x2 -> x0, other arithmetic: 5.69 us -> none  [the longest x1 5.67 us: on_device(): (slot_ids % slot_depth < block_count[slot_ids // slot_depth]).astype(jnp....]
  transfers between devices with their start and end apart: 1 -> 1, of which waited for: 0 -> 1; matrix products, arithmetic and copies ran while one was open for 13% -> 0% of each run, Pallas kernels for 0% -> 2%
where the time goes in v1:
time: 56.8 us; the launch traced here: 56.5 us
  waiting for transfers between devices  18.3 us (32%)
  blocking collectives  14.6 us (26%)
  Pallas kernels  11.3 us (20%)
  starting transfers between devices  7.43 us (13%)
  local copies, waits for them, and re-layouts  4.79 us (8%)
    all_to_all x1, waiting for transfers between devices, on_device(): arrived = lax.all_to_all(payload, 'aux', 0, 0, tiled=True)  18.3 us
    all_to_all x1, blocking collectives, on_device(): partial = lax.all_to_all(partial, 'aux', 0, 0, tiled=True)  14.6 us
    pallas_call x1, Pallas kernels, on_device(): pl.pallas_call(functools.partial(density_kernel, owners, depth), out_shap...  7.61 us
    all_to_all x1, starting transfers between devices, on_device(): arrived = lax.all_to_all(payload, 'aux', 0, 0, tiled=True)  7.43 us
    unnamed x18, local copies, waits for them, and re-layouts  4.79 us
    pallas_call x1, Pallas kernels, on_device(): pl.pallas_call(functools.partial(finish_kernel, components, aux_local, au...  1.66 us
  transfers between devices with their start and end apart: 1, of which 1 were waited for; matrix products, arithmetic and copies ran while one was open for 0% of the time, Pallas kernels for 2%

profile of v1, /device:TPU:0, one launch (start us, length us, event | category | flops | bytes accessed | tf_op | source)
XLA Modules:
  0.0 56.5 jit_solution(9714489157218873791)
XLA Ops:
  0.0 0.0 copy-start.4
  0.0 0.0 copy-start.7
  0.0 0.0 copy-start.6
  0.0 0.0 copy-start.5
  0.0 0.0 copy-start.3
  0.0 7.6 %density.1 = (bf16[16,128,256]{2,1,0:T(8,128)(2,1)}, f32[8,128]{1,0:T(8,128)}) custom-call(bf16[4,256,256]{2,1,0:T(8,128)(2,1)} %refs_0_.2, bf16[256,256]{1,0:T(8,128)(2,1)} %refs_1_.2, bf16[256,256]{1,0:T(8,128)(2,1)} %refs_2_.1, bf16[256,256]{1,0:T(8,128)(2,1)} %refs_3_.2, bf16[256,256]{1,0:T(8,128)(2,1)} %refs_4_.2, s32[1,512]{1,0:T(1,128)} %bitcast.2), custom_call_target="tpu_custom_call" | custom-call | flops 1073741824 | bytes 2097152 | tf_op jit(solution)/shard_map/density/pallas_call | solution.py:230
  7.6 7.4 %all-to-all-start = ((bf16[16,128,256]{2,1,0:T(8,128)(2,1)}), bf16[16,128,256]{2,1,0:T(8,128)(2,1)S(1)}, u32[]{:S(2)}, u32[]{:S(2)}) async-start(bf16[16,128,256]{2,1,0:T(8,128)(2,1)} %get-tuple-element.12), calls=%async_computation | async-start | bytes 2097152 | tf_op jit(solution)/shard_map/all_to_all | solution.py:255
  15.1 0.0 copy-done.4
  15.1 0.0 copy-done.7
  15.1 0.0 copy-done.6
  15.1 0.0 copy-done.5
  15.1 0.0 copy-done.3
  15.1 0.0 copy-start.2
  15.1 1.9 %copy-done.2 = bf16[3,64,32,256]{3,2,1,0:T(8,128)(2,1)S(1)} copy-done((bf16[3,64,32,256]{3,2,1,0:T(8,128)(2,1)S(1)}, bf16[3,64,32,256]{3,2,1,0:T(8,128)(2,1)}, u32[]{:S(2)}) %copy-start.2) | copy-done | bytes 3145752
  17.0 0.0 copy-start.8
  17.0 0.7 %copy-done.8 = f32[8,128]{1,0:T(8,128)S(1)} copy-done((f32[8,128]{1,0:T(8,128)S(1)}, f32[8,128]{1,0:T(8,128)}, u32[]{:S(2)}) %copy-start.8) | copy-done | bytes 4120
  17.7 1.0 %prepare.1 = (bf16[64,32,256]{2,1,0:T(8,128)(2,1)S(1)}, bf16[64,32,256]{2,1,0:T(8,128)(2,1)S(1)}, bf16[64,32,256]{2,1,0:T(8,128)(2,1)S(1)}, s32[32,256]{1,0:T(8,128)S(1)}, f32[16,128]{1,0:T(8,128)S(1)}) custom-call(bf16[3,64,32,256]{3,2,1,0:T(8,128)(2,1)S(1)} %copy-done.2, bf16[3,4,64]{2,1,0:T(4,128)(2,1)S(1)} %copy-done.3, s32[1,256]{1,0:T(1,128)S(1)} %bitcast.3, ...), custom_call_target="tpu_custom_call" | custom-call | flops 1073741824 | bytes 4194304 | tf_op jit(solution)/shard_map/prepare/pallas_call | solution.py:256
  18.7 0.0 copy-start
  18.7 1.0 %copy-done = bf16[64,32,256]{2,1,0:T(8,128)(2,1)} copy-done((bf16[64,32,256]{2,1,0:T(8,128)(2,1)}, bf16[64,32,256]{2,1,0:T(8,128)(2,1)S(1)}, u32[]{:S(2)}) %copy-start) | copy-done | bytes 1048600
  19.7 18.3 %all-to-all-done.arrived = bf16[16,128,256]{2,1,0:T(8,128)(2,1)S(1)} async-done(((bf16[16,128,256]{2,1,0:T(8,128)(2,1)}), bf16[16,128,256]{2,1,0:T(8,128)(2,1)S(1)}, u32[]{:S(2)}, u32[]{:S(2)}) %all-to-all-start) | async-done | bytes 1048608 | tf_op jit(solution)/shard_map/all_to_all | solution.py:255
  38.0 0.0 copy-start.1
  38.0 1.2 %copy-done.1 = bf16[64,32,256]{2,1,0:T(8,128)(2,1)S(1)} copy-done((bf16[64,32,256]{2,1,0:T(8,128)(2,1)S(1)}, bf16[64,32,256]{2,1,0:T(8,128)(2,1)}, u32[]{:S(2)}) %copy-start.1) | copy-done | bytes 1048600
  39.2 1.0 %gradient.1 = f32[16,16,128]{2,1,0:T(8,128)S(1)} custom-call(bf16[16,128,256]{2,1,0:T(8,128)(2,1)S(1)} %all-to-all-done.arrived, bf16[64,32,256]{2,1,0:T(8,128)(2,1)S(1)} %get-tuple-element.14.refs_0_, bf16[64,32,256]{2,1,0:T(8,128)(2,1)S(1)} %get-tuple-element.15.refs_1_, bf16[64,32,256]{2,1,0:T(8,128)(2,1)S(1)} %copy-done.1, ...), custom_call_target="tpu_custom_call" | custom-call | tf_op jit(solution)/shard_map/gradient/pallas_call | solution.py:278
  40.2 14.6 %all_to_all.10.arrived = f32[16,16,128]{2,1,0:T(8,128)} all-to-all(f32[16,16,128]{2,1,0:T(8,128)S(1)} %gradient.1), channel_id=1, replica_groups=mesh['grp'=2,'aux'=16] {'aux'}, dimensions={0} | all-to-all | bytes 262144 | tf_op jit(solution)/shard_map/all_to_all | solution.py:286
  54.8 1.7 %finish.1 = f32[3,32]{1,0:T(4,128)} custom-call(f32[16,16,128]{2,1,0:T(8,128)} %all_to_all.10.arrived), custom_call_target="tpu_custom_call" | custom-call | tf_op jit(solution)/shard_map/finish/pallas_call | solution.py:287
Async XLA Ops:
  0.0 15.1 %copy-start.4 = (s32[512]{0:T(512)S(1)}, s32[512]{0:T(512)}, u32[]{:S(2)}) copy-start(s32[512]{0:T(512)} %refs_4_.3) | copy-start | bytes 6148
  0.0 15.1 %copy-start.7 = (s32[16]{0:T(128)S(1)}, s32[16]{0:T(128)}, u32[]{:S(2)}) copy-start(s32[16]{0:T(128)} %refs_5_.1) | copy-start | bytes 196
  0.0 15.1 %copy-start.6 = (s32[4]{0:T(128)S(1)}, s32[4]{0:T(128)}, u32[]{:S(2)}) copy-start(s32[4]{0:T(128)} %refs_3_.3) | copy-start | bytes 52
  0.0 15.1 %copy-start.5 = (s32[256]{0:T(256)S(1)}, s32[256]{0:T(256)}, u32[]{:S(2)}) copy-start(s32[256]{0:T(256)} %param.18) | copy-start | bytes 3076
  0.0 15.1 %copy-start.3 = (bf16[3,4,64]{2,1,0:T(4,128)(2,1)S(1)}, bf16[3,4,64]{2,1,0:T(4,128)(2,1)}, u32[]{:S(2)}) copy-start(bf16[3,4,64]{2,1,0:T(4,128)(2,1)} %refs_1_.3) | copy-start | bytes 4612
  7.6 30.3 %all-to-all-start = ((bf16[16,128,256]{2,1,0:T(8,128)(2,1)}), bf16[16,128,256]{2,1,0:T(8,128)(2,1)S(1)}, u32[]{:S(2)}, u32[]{:S(2)}) async-start(bf16[16,128,256]{2,1,0:T(8,128)(2,1)} %get-tuple-element.12), calls=%async_computation | async-start | bytes 2097152 | tf_op jit(solution)/shard_map/all_to_all | solution.py:255
  15.1 1.9 %copy-start.2 = (bf16[3,64,32,256]{3,2,1,0:T(8,128)(2,1)S(1)}, bf16[3,64,32,256]{3,2,1,0:T(8,128)(2,1)}, u32[]{:S(2)}) copy-start(bf16[3,64,32,256]{3,2,1,0:T(8,128)(2,1)} %refs_0_.3) | copy-start | bytes 9437188
  17.0 0.7 %copy-start.8 = (f32[8,128]{1,0:T(8,128)S(1)}, f32[8,128]{1,0:T(8,128)}, u32[]{:S(2)}) copy-start(f32[8,128]{1,0:T(8,128)} %get-tuple-element.13.refs_6_) | copy-start | bytes 12292
  18.7 1.0 %copy-start = (bf16[64,32,256]{2,1,0:T(8,128)(2,1)}, bf16[64,32,256]{2,1,0:T(8,128)(2,1)S(1)}, u32[]{:S(2)}) copy-start(bf16[64,32,256]{2,1,0:T(8,128)(2,1)S(1)} %get-tuple-element.16.refs_2_) | copy-start | bytes 3145732
  38.0 1.2 %copy-start.1 = (bf16[64,32,256]{2,1,0:T(8,128)(2,1)S(1)}, bf16[64,32,256]{2,1,0:T(8,128)(2,1)}, u32[]{:S(2)}) copy-start(bf16[64,32,256]{2,1,0:T(8,128)(2,1)} %copy-done) | copy-start | bytes 3145732
